TPU v7x, 32 devices: a whole 2x2x4 slice. The times are simulated.
32 devices in a mesh: grp: 2 (over x), az: 8 (over z, y), ax: 2 (over core).
Axes of the slice: x: 2, y: 2, z: 4, core: 2. Of those that a mesh axis runs over, the one named last changes fastest.
Arguments:
- cavity_block: float32 [8, 96, 32, 256], P(None, 'grp', 'az', 'ax'), may hold values from -95 to 95
- shell_block: float32 [8, 6, 32, 256], P(None, None, 'az', 'ax'), may hold values from -95 to 95
- column_matrix: float32 [2, 48, 48], P('grp'), may hold values from -2 to 6, as said below
- shell_matrix: float32 [6, 6], replicated, may hold values from -2 to 6, as said below
- shifted_diagonal: float32 [96, 32, 256], P('grp', 'az', 'ax'), may hold values from 1.6 to 3
- shell_diagonal: float32 [6, 32, 256], P(None, 'az', 'ax'), may hold values from 1.6 to 3
- wet_area: float32 [32, 256], P('az', 'ax'), may hold values from 0.3 to 1.5
Outputs:
- cavity_solution: float32 [8, 96, 32, 256], P(None, 'grp', 'az', 'ax')
- cavity_residual: float32 [8, 96, 32, 256], P(None, 'grp', 'az', 'ax')
- shell_solution: float32 [8, 6, 32, 256], P(None, None, 'az', 'ax')
- shell_residual: float32 [8, 6, 32, 256], P(None, None, 'az', 'ax')
Inputs may be any that keep to these rules, and one draw needn't show every extreme that they name: `column_matrix`: each symmetric and positive definite. `shell_matrix`: symmetric and positive definite.
All inputs are finite; a program needn't handle non-finite values.
Results may differ from a plain program's by a relative error of at most 0.0015.
Values sent between devices are 32-bit elements; how exact they have to be, the bound alone decides.
No kernel may reach another device: no remote copies, remote signals or barrier semaphores. Data moves between devices by JAX's collectives and lax.ppermute only.
A program may use at most 128 MiB of HBM per device.

v0:
```python
import jax
import jax.numpy as jnp
from jax import lax
from jax.sharding import PartitionSpec as P

ITERS = 3
exact_mode = lax.Precision.HIGHEST


def swapped(block, axis, apart):
    count = lax.axis_size(axis)
    route = []
    for low in range(count):
        high = low | 1 << apart
        if high != low and high < count:
            route += [(low, high), (high, low)]
    return lax.ppermute(block, axis, route)


def extended(array, sides, width, wrap):
    for axis, dim in sides:
        peers, length = (lax.axis_size(axis), array.shape[dim])
        up = [(i, (i + 1) % peers) for i in range(peers if wrap else peers - 1)]
        down = [(j, i) for i, j in up]
        last = lax.slice_in_dim(array, length - width, length, axis=dim)
        first = lax.slice_in_dim(array, 0, width, axis=dim)
        before = lax.ppermute(last, axis, up)
        after = lax.ppermute(first, axis, down)
        array = jnp.concatenate([before, array, after], axis=dim)
    return array


def solve_posdef(gram_matrix, targets):
    factor = jnp.linalg.cholesky(gram_matrix)
    middle = lax.linalg.triangular_solve(factor, targets, left_side=True, lower=True)
    return lax.linalg.triangular_solve(factor, middle, left_side=True, lower=True, transpose_a=True)


def products(first_set, second_set):
    return jnp.einsum("vrax,wrax->vw", first_set, second_set, precision=exact_mode)


def combine(vector_set, mixing):
    return jnp.einsum("vrax,vw->wrax", vector_set, mixing, precision=exact_mode)


def column_part(vector_set, matrix):
    flat_set = vector_set.reshape(vector_set.shape[0], vector_set.shape[1], -1)
    mixed_set = jnp.einsum("rs,vsc->vrc", matrix, flat_set, precision=exact_mode)
    return mixed_set.reshape(vector_set.shape)


def coupled(result, vector_set, wet_area, layout):
    half, interface_row, outer_flag = layout
    iface_own = lax.dynamic_slice_in_dim(vector_set, interface_row, 1, 1)
    wall_own = vector_set[:, half - 1 : half]
    sent = jnp.concatenate([iface_own, wall_own], axis=1)
    received = swapped(sent, "grp", 0)
    result_row = lax.dynamic_slice_in_dim(result, interface_row, 1, 1)
    result = lax.dynamic_update_slice_in_dim(
        result, result_row - received[:, 0:1], interface_row, 1
    )
    wall = outer_flag * wall_own + (1.0 - outer_flag) * received[:, 1:2]
    shell_top = vector_set[:, half : half + 1]
    result = result.at[:, half - 1 : half].add(-outer_flag * wet_area * shell_top)
    result = result.at[:, half : half + 1].add(-wet_area * wall)
    return result


def apply_shallow(vector_set, matrix, diagonal_set, wet_area, layout):
    beside_all = extended(vector_set, (("az", 2),), 1, True)
    along = extended(vector_set, (("ax", 3),), 1, False)
    neighbours = beside_all[:, :, 2:] + beside_all[:, :, :-2] + along[..., 2:] + along[..., :-2]
    result = column_part(vector_set, matrix) + (4.0 + diagonal_set) * vector_set - neighbours
    return coupled(result, vector_set, wet_area, layout)


def per_device(
    cavity_block,
    shell_block,
    column_matrix,
    shell_matrix,
    shifted_diagonal,
    shell_diagonal,
    wet_area,
):
    group_index = lax.axis_index("grp")
    outer_flag = (group_index == 1).astype(jnp.float32)
    shell_share = 1.0 - outer_flag
    half = column_matrix.shape[1]
    shell_rows = shell_matrix.shape[0]
    interface_row = jnp.where(group_index == 1, 0, half - 1).astype(jnp.int32)
    layout = (half, interface_row, outer_flag)
    upper = jnp.concatenate([column_matrix[0], jnp.zeros((half, shell_rows), jnp.float32)], axis=1)
    lower = jnp.concatenate([jnp.zeros((shell_rows, half), jnp.float32), shell_matrix], axis=1)
    matrix = jnp.concatenate([upper, lower], axis=0)
    right_side = jnp.concatenate([cavity_block, shell_block], axis=1)
    diagonal_own = jnp.concatenate([shifted_diagonal, shell_diagonal], axis=0)

    def moments_local(first_set, second_set):
        cavity_part = products(first_set[:, :half], second_set[:, :half])
        return cavity_part + shell_share * products(first_set[:, half:], second_set[:, half:])

    residual = right_side
    direction = right_side
    solution = jnp.zeros_like(right_side)
    start_core = residual
    norms_now = lax.psum(moments_local(start_core, start_core), ("grp", "az", "ax"))
    for sweep in range(ITERS):
        image_set = apply_shallow(direction, matrix, diagonal_own, wet_area, layout)
        direction_core = direction
        residual_core = residual
        curvature, crossing, squares = lax.psum(
            (
                moments_local(direction_core, image_set),
                moments_local(image_set, residual_core),
                moments_local(image_set, image_set),
            ),
            ("grp", "az", "ax"),
        )
        step_mix = solve_posdef(curvature, norms_now)
        norms_next = norms_now - jnp.dot(step_mix.T, crossing, precision=exact_mode)
        norms_next = norms_next - jnp.dot(crossing.T, step_mix, precision=exact_mode)
        norms_next = norms_next + jnp.dot(
            jnp.dot(step_mix.T, squares, precision=exact_mode), step_mix, precision=exact_mode
        )
        solution = solution + combine(direction_core, step_mix)
        residual = residual - combine(image_set, step_mix)
        if sweep + 1 < ITERS:
            turn_mix = solve_posdef(norms_now, norms_next)
            direction = residual + combine(direction, turn_mix)
            norms_now = norms_next
    return (solution[:, :half], residual[:, :half], solution[:, half:], residual[:, half:])


def solution(mesh):
    return jax.shard_map(
        per_device,
        mesh=mesh,
        in_specs=(
            P(None, "grp", "az", "ax"),
            P(None, None, "az", "ax"),
            P("grp", None, None),
            P(),
            P("grp", "az", "ax"),
            P(None, "az", "ax"),
            P("az", "ax"),
        ),
        out_specs=(
            P(None, "grp", "az", "ax"),
            P(None, "grp", "az", "ax"),
            P(None, None, "az", "ax"),
            P(None, None, "az", "ax"),
        ),
        check_vma=False,
    )
```

profile of v0, /device:TPU:0, one launch (start us, length us, event | category | flops | bytes accessed | tf_op | source)
XLA Modules:
  0.0 250.7 jit_solution(17498085943303923312)
XLA Ops:
  0.6 2.5 fusion.124
  5.1 2.4 collective-permute-start.3
  7.9 1.3 collective-permute-start.2
  10.0 2.3 collective-permute-start.1
  12.3 3.0 %collective-permute-start = (f32[8,54,1,128]{3,0,1,2:T(8,128)}, f32[8,54,1,128]{3,0,1,2:T(8,128)}, u32[]{:S(2)}, u32[]{:S(2)}) collective-permute-start(f32[8,54,1,128]{3,0,1,2:T(8,128)} %get-tuple-element.110), channel_id=1, source_target_pairs={{2,0},{4,2},{6,4},{8,6},{10,8},{12,10},{14,12},{0,14},{3,1},{5,3},... | collective-permute-start | bytes 663560 | tf_op jit(solution)/shard_map/ppermute | solution.py:28
  16.7 1.7 collective-permute-start.4
  18.4 1.9 convolution_bitcast_fusion.3
  21.4 2.4 convolution_bitcast_fusion.2
  24.9 1.4 copy.165
  26.3 2.5 fusion.26
  31.0 1.9 convolution_bitcast_fusion.15
  32.9 1.8 convolution_bitcast_fusion.13
  35.7 38.6 %all-reduce.3 = (f32[8,8]{0,1:T(8,128)S(1)}, f32[8,8]{1,0:T(8,128)S(1)}, f32[8,8]{0,1:T(8,128)S(1)}, f32[8,8]{0,1:T(8,128)S(1)}) all-reduce(f32[8,8]{0,1:T(8,128)S(1)} %copy-done.18, f32[8,8]{1,0:T(8,128)S(1)} %bitcast.241, f32[8,8]{0,1:T(8,128)S(1)} %fusion.11, ...), channel_id=1, replica_groups=mesh['grp'=2,'az'=8,'ax'=2] {'grp','az','ax'}, use_global_device_ids=true, to_apply=%region_3.0 | all-reduce | flops 256 | bytes 2048 | tf_op jit(solution)/shard_map/psum | solution.py:108
  77.5 1.9 fusion.31
  85.0 1.2 fusion.121
  88.4 2.1 copy.206
  90.6 1.9 collective-permute-start.8
  93.4 1.3 collective-permute-start.7
  94.7 2.4 collective-permute-start.6
  97.1 2.4 collective-permute-start.5
  99.5 3.1 %convolution_bitcast_fusion.1 = f32[8,54,512]{2,1,0:T(8,128)} fusion(f32[8,54,512]{2,0,1:T(8,128)S(1)} %bitcast.235, f32[6,6]{1,0:T(8,128)S(1)} %copy-done.14, f32[48,48]{1,0:T(8,128)} %bitcast.238), kind=kOutput, calls=%fused_computation.1 | convolution fusion | flops 143341808 | bytes 1778832 | tf_op jit(solution)/shard_map/rs,vsc->vrc/dot_general | solution.py:49
  103.3 2.3 collective-permute-start.9
  107.6 1.2 custom-call.23
  108.9 1.1 copy.207
  110.0 1.3 copy.205
  112.0 2.5 fusion.22
  116.0 1.8 convolution_bitcast_fusion.11
  117.8 1.8 convolution_bitcast_fusion.9
  119.6 1.8 convolution_bitcast_fusion.7
  122.3 37.7 %all-reduce.2 = (f32[8,8]{0,1:T(8,128)S(1)}, f32[8,8]{0,1:T(8,128)}, f32[8,8]{0,1:T(8,128)}) all-reduce(f32[8,8]{0,1:T(8,128)S(1)} %fusion.7, f32[8,8]{0,1:T(8,128)S(1)} %fusion.5, f32[8,8]{0,1:T(8,128)S(1)} %fusion.3), channel_id=1, replica_groups=mesh['grp'=2,'az'=8,'ax'=2] {'grp','az','ax'}, use_global_device_ids=true, to_apply=%region_6.10 | all-reduce | flops 192 | bytes 1536 | tf_op jit(solution)/shard_map/psum | solution.py:113
  166.8 1.5 fusion.119
  170.3 1.9 convolution_add_fusion.2
  172.1 2.2 copy.237
  174.4 2.0 collective-permute-start.13
  177.3 1.3 collective-permute-start.12
  178.6 2.7 %collective-permute-start.11 = (f32[8,54,1,128]{3,0,1,2:T(8,128)}, f32[8,54,1,128]{3,0,1,2:T(8,128)S(1)}, u32[]{:S(2)}, u32[]{:S(2)}) collective-permute-start(f32[8,54,1,128]{3,0,1,2:T(8,128)} %get-tuple-element.101), channel_id=1, source_target_pairs={{0,2},{2,4},{4,6},{6,8},{8,10},{10,12},{12,14},{14,0},{1,3},{3,5},... | collective-permute-start | bytes 663560 | tf_op jit(solution)/shard_map/ppermute | solution.py:27
  181.3 2.1 collective-permute-start.10
  183.4 3.1 %convolution_bitcast_fusion = f32[8,54,512]{2,1,0:T(8,128)} fusion(f32[8,54,512]{2,0,1:T(8,128)S(1)} %bitcast.236, f32[6,6]{1,0:T(8,128)S(1)} %copy-done.14, f32[48,48]{1,0:T(8,128)} %bitcast.239), kind=kOutput, calls=%fused_computation | convolution fusion | flops 143341808 | bytes 1778832 | tf_op jit(solution)/shard_map/rs,vsc->vrc/dot_general | solution.py:49
  187.1 2.2 collective-permute-start.14
  189.3 1.1 copy.238
  190.5 1.3 copy.236
  192.7 1.8 collective-permute-done.10
  194.5 2.4 fusion.18
  198.5 1.8 convolution_bitcast_fusion.5
  200.5 38.7 %psum.63 = f32[8,8]{0,1:T(8,128)S(1)} all-reduce(f32[8,8]{0,1:T(8,128)S(1)} %fusion.1), channel_id=1, replica_groups=mesh['grp'=2,'az'=8,'ax'=2] {'grp','az','ax'}, use_global_device_ids=true, to_apply=%region_9.13 | all-reduce | flops 64 | bytes 512 | tf_op jit(solution)/shard_map/psum | solution.py:113
  245.4 1.1 slice-done.2
  246.6 1.1 copy.249
  247.8 1.4 copy.250
  (165 shorter events, 48.5 us)
Async XLA Ops:
  0.6 2.5 %copy-start.6 = (f32[8,6,4,128]{3,2,1,0:T(4,128)S(1)}, f32[8,6,4,128]{3,2,1,0:T(4,128)}, u32[]{:S(2)}) copy-start(f32[8,6,4,128]{3,2,1,0:T(4,128)} %param.25) | copy-start | bytes 294916
  5.1 19.4 %collective-permute-start.3 = (f32[8,54,4,1]{1,0,3,2:T(8,128)}, f32[8,54,4,1]{1,0,3,2:T(8,128)S(1)}, u32[]{:S(2)}, u32[]{:S(2)}) collective-permute-start(f32[8,54,4,1]{1,0,3,2:T(8,128)} %copy.166), channel_id=1, source_target_pairs={{0,1},{2,3},{4,5},{6,7},{8,9},{10,11},{12,13},{14,15},{16,17},{18,... | collective-permute-start | bytes 20744 | tf_op jit(solution)/shard_map/ppermute | solution.py:27
  7.5 10.9 %copy-start = (f32[8,48,4,128]{3,2,1,0:T(4,128)S(1)}, f32[8,48,4,128]{3,2,1,0:T(4,128)}, u32[]{:S(2)}) copy-start(f32[8,48,4,128]{3,2,1,0:T(4,128)} %param.24) | copy-start | bytes 2359300
  7.9 17.0 %collective-permute-start.2 = (f32[8,54,4,1]{1,0,3,2:T(8,128)S(1)}, f32[8,54,4,1]{1,0,3,2:T(8,128)S(1)}, u32[]{:S(2)}, u32[]{:S(2)}) collective-permute-start(f32[8,54,4,1]{1,0,3,2:T(8,128)S(1)} %copy.164), channel_id=1, source_target_pairs={{1,0},{3,2},{5,4},{7,6},{9,8},{11,10},{13,12},{15,14},{17,16},{19,... | collective-permute-start | bytes 20744 | tf_op jit(solution)/shard_map/ppermute | solution.py:28
  10.0 16.3 %collective-permute-start.1 = (f32[8,54,1,128]{3,0,1,2:T(8,128)}, f32[8,54,1,128]{3,0,1,2:T(8,128)}, u32[]{:S(2)}, u32[]{:S(2)}) collective-permute-start(f32[8,54,1,128]{3,0,1,2:T(8,128)} %get-tuple-element.111), channel_id=1, source_target_pairs={{0,2},{2,4},{4,6},{6,8},{8,10},{10,12},{12,14},{14,0},{1,3},{3,5},... | collective-permute-start | bytes 663560 | tf_op jit(solution)/shard_map/ppermute | solution.py:27
  12.3 14.0 %collective-permute-start = (f32[8,54,1,128]{3,0,1,2:T(8,128)}, f32[8,54,1,128]{3,0,1,2:T(8,128)}, u32[]{:S(2)}, u32[]{:S(2)}) collective-permute-start(f32[8,54,1,128]{3,0,1,2:T(8,128)} %get-tuple-element.110), channel_id=1, source_target_pairs={{2,0},{4,2},{6,4},{8,6},{10,8},{12,10},{14,12},{0,14},{3,1},{5,3},... | collective-permute-start | bytes 663560 | tf_op jit(solution)/shard_map/ppermute | solution.py:28
  16.7 12.1 %collective-permute-start.4 = (f32[8,2,4,128]{3,0,1,2:T(8,128)}, f32[8,2,4,128]{3,0,1,2:T(8,128)}, u32[]{:S(2)}, u32[]{:S(2)}) collective-permute-start(f32[8,2,4,128]{3,0,1,2:T(8,128)} %pad_maximum_fusion.12), channel_id=1, source_target_pairs={{0,16},{16,0},{1,17},{17,1},{2,18},{18,2},{3,19},{19,3},{4,20},{20... | collective-permute-start | bytes 98312 | tf_op jit(solution)/shard_map/ppermute | solution.py:17
  20.4 0.9 copy-start.8
  20.4 0.9 copy-start.14
  21.3 2.4 copy-start.21
  21.3 2.4 copy-start.11
  21.4 2.4 copy-start.19
  32.9 1.8 copy-start.7
  34.9 0.7 copy-start.18
  90.6 18.3 %collective-permute-start.8 = (f32[8,54,4,1]{1,0,3,2:T(8,128)}, f32[8,54,4,1]{1,0,3,2:T(8,128)}, u32[]{:S(2)}, u32[]{:S(2)}) collective-permute-start(f32[8,54,4,1]{1,0,3,2:T(8,128)} %copy.206), channel_id=1, source_target_pairs={{0,1},{2,3},{4,5},{6,7},{8,9},{10,11},{12,13},{14,15},{16,17},{18,... | collective-permute-start | bytes 20744 | tf_op jit(solution)/shard_map/ppermute | solution.py:27
  93.4 16.6 %collective-permute-start.7 = (f32[8,54,4,1]{1,0,3,2:T(8,128)}, f32[8,54,4,1]{1,0,3,2:T(8,128)S(1)}, u32[]{:S(2)}, u32[]{:S(2)}) collective-permute-start(f32[8,54,4,1]{1,0,3,2:T(8,128)} %copy.204), channel_id=1, source_target_pairs={{1,0},{3,2},{5,4},{7,6},{9,8},{11,10},{13,12},{15,14},{17,16},{19,... | collective-permute-start | bytes 20744 | tf_op jit(solution)/shard_map/ppermute | solution.py:28
  94.7 16.6 %collective-permute-start.6 = (f32[8,54,1,128]{3,0,1,2:T(8,128)}, f32[8,54,1,128]{3,0,1,2:T(8,128)S(1)}, u32[]{:S(2)}, u32[]{:S(2)}) collective-permute-start(f32[8,54,1,128]{3,0,1,2:T(8,128)} %get-tuple-element.107), channel_id=1, source_target_pairs={{0,2},{2,4},{4,6},{6,8},{8,10},{10,12},{12,14},{14,0},{1,3},{3,5},... | collective-permute-start | bytes 663560 | tf_op jit(solution)/shard_map/ppermute | solution.py:27
  97.1 14.9 %collective-permute-start.5 = (f32[8,54,1,128]{3,0,1,2:T(8,128)}, f32[8,54,1,128]{3,0,1,2:T(8,128)}, u32[]{:S(2)}, u32[]{:S(2)}) collective-permute-start(f32[8,54,1,128]{3,0,1,2:T(8,128)} %get-tuple-element.106), channel_id=1, source_target_pairs={{2,0},{4,2},{6,4},{8,6},{10,8},{12,10},{14,12},{0,14},{3,1},{5,3},... | collective-permute-start | bytes 663560 | tf_op jit(solution)/shard_map/ppermute | solution.py:28
  99.5 3.2 %copy-start.12 = (f32[8,1,4,128]{3,0,1,2:T(8,128)S(1)}, f32[8,1,4,128]{3,0,1,2:T(8,128)}, u32[]{:S(2)}) copy-start(f32[8,1,4,128]{3,0,1,2:T(8,128)} %get-tuple-element.104) | copy-start | bytes 49156
  99.5 3.2 %copy-start.13 = (f32[8,1,4,128]{3,0,1,2:T(8,128)S(1)}, f32[8,1,4,128]{3,0,1,2:T(8,128)}, u32[]{:S(2)}) copy-start(f32[8,1,4,128]{3,0,1,2:T(8,128)} %get-tuple-element.105) | copy-start | bytes 49156
  102.7 2.9 %copy-start.16 = (f32[8,8]{1,0:T(8,128)S(1)}, f32[8,8]{1,0:T(8,128)}, u32[]{:S(2)}) copy-start(f32[8,8]{1,0:T(8,128)} %copy.218) | copy-start | bytes 772
  103.3 11.2 %collective-permute-start.9 = (f32[8,2,4,128]{3,0,1,2:T(8,128)}, f32[8,2,4,128]{3,0,1,2:T(8,128)}, u32[]{:S(2)}, u32[]{:S(2)}) collective-permute-start(f32[8,2,4,128]{3,0,1,2:T(8,128)} %pad_maximum_fusion.13), channel_id=1, source_target_pairs={{0,16},{16,0},{1,17},{17,1},{2,18},{18,2},{3,19},{19,3},{4,20},{20... | collective-permute-start | bytes 98312 | tf_op jit(solution)/shard_map/ppermute | solution.py:17
  111.3 0.7 copy-start.9
  163.1 0.9 copy-start.17
  164.0 0.7 copy-start.20
  164.9 0.7 copy-start.15
  169.1 1.2 copy-start.2
  172.1 4.2 %copy-start.1 = (f32[8,54,4,1]{3,0,1,2:T(8,128)S(1)}, f32[8,54,4,1]{3,0,1,2:T(8,128)}, u32[]{:S(2)}) copy-start(f32[8,54,4,1]{3,0,1,2:T(8,128)} %get-tuple-element.102) | copy-start | bytes 20740
  174.4 15.0 %collective-permute-start.13 = (f32[8,54,4,1]{1,0,3,2:T(8,128)}, f32[8,54,4,1]{1,0,3,2:T(8,128)}, u32[]{:S(2)}, u32[]{:S(2)}) collective-permute-start(f32[8,54,4,1]{1,0,3,2:T(8,128)} %copy.237), channel_id=1, source_target_pairs={{0,1},{2,3},{4,5},{6,7},{8,9},{10,11},{12,13},{14,15},{16,17},{18,... | collective-permute-start | bytes 20744 | tf_op jit(solution)/shard_map/ppermute | solution.py:27
  177.3 13.2 %collective-permute-start.12 = (f32[8,54,4,1]{1,0,3,2:T(8,128)}, f32[8,54,4,1]{1,0,3,2:T(8,128)S(1)}, u32[]{:S(2)}, u32[]{:S(2)}) collective-permute-start(f32[8,54,4,1]{1,0,3,2:T(8,128)} %copy.235), channel_id=1, source_target_pairs={{1,0},{3,2},{5,4},{7,6},{9,8},{11,10},{13,12},{15,14},{17,16},{19,... | collective-permute-start | bytes 20744 | tf_op jit(solution)/shard_map/ppermute | solution.py:28
  178.6 13.4 %collective-permute-start.11 = (f32[8,54,1,128]{3,0,1,2:T(8,128)}, f32[8,54,1,128]{3,0,1,2:T(8,128)S(1)}, u32[]{:S(2)}, u32[]{:S(2)}) collective-permute-start(f32[8,54,1,128]{3,0,1,2:T(8,128)} %get-tuple-element.101), channel_id=1, source_target_pairs={{0,2},{2,4},{4,6},{6,8},{8,10},{10,12},{12,14},{14,0},{1,3},{3,5},... | collective-permute-start | bytes 663560 | tf_op jit(solution)/shard_map/ppermute | solution.py:27
  181.3 13.2 %collective-permute-start.10 = (f32[8,54,1,128]{3,0,1,2:T(8,128)}, f32[8,54,1,128]{3,0,1,2:T(8,128)}, u32[]{:S(2)}, u32[]{:S(2)}) collective-permute-start(f32[8,54,1,128]{3,0,1,2:T(8,128)} %get-tuple-element.100), channel_id=1, source_target_pairs={{2,0},{4,2},{6,4},{8,6},{10,8},{12,10},{14,12},{0,14},{3,1},{5,3},... | collective-permute-start | bytes 663560 | tf_op jit(solution)/shard_map/ppermute | solution.py:28
  187.1 9.8 %collective-permute-start.14 = (f32[8,2,4,128]{3,0,1,2:T(8,128)}, f32[8,2,4,128]{3,0,1,2:T(8,128)}, u32[]{:S(2)}, u32[]{:S(2)}) collective-permute-start(f32[8,2,4,128]{3,0,1,2:T(8,128)} %pad_maximum_fusion.14), channel_id=1, source_target_pairs={{0,16},{16,0},{1,17},{17,1},{2,18},{18,2},{3,19},{19,3},{4,20},{20... | collective-permute-start | bytes 98312 | tf_op jit(solution)/shard_map/ppermute | solution.py:17
  192.0 0.7 copy-start.10
  242.4 1.2 copy-start.5
  243.6 1.8 copy-start.3
  244.5 1.0 copy-start.4
  245.4 1.1 slice-start.2
  246.6 1.2 slice-start
  247.8 1.4 slice-start.3
  249.2 0.9 slice-start.1
where the time goes:
time: 252 us; the launch traced here: 251 us
  blocking collectives  115 us (46%)
  local copies, waits for them, and re-layouts  36.6 us (15%)
  matrix products  36.5 us (14%)
  starting transfers between devices  31.1 us (12%)
  other arithmetic  28.4 us (11%)
    psum x2, blocking collectives, per_device(): lax.psum((moments_local(direction_core, image_set), moments_local(image_s...  76.4 us
    psum x1, blocking collectives, per_device(): lax.psum(moments_local(start_core, start_core), ('grp', 'az', 'ax'))  38.6 us
    dot_general x14, matrix products, products(): jnp.einsum('vrax,wrax->vw', first_set, second_set, precision=exact_mode)  15.5 us
    ppermute x6, starting transfers between devices, extended(): before = lax.ppermute(last, axis, up)  13.6 us
    unnamed x50, local copies, waits for them, and re-layouts  12 us
    ppermute x6, starting transfers between devices, extended(): after = lax.ppermute(first, axis, down)  11.4 us
    dot_general x8, matrix products, combine(): return jnp.einsum('vrax,vw->wrax', vector_set, mixing, precision=exact_mode)  9.04 us
    dot_general x3, matrix products, column_part(): jnp.einsum('rs,vsc->vrc', matrix, flat_set, precision=exact_mode)  8.66 us
  transfers between devices with their start and end apart: 15, of which 2 were waited for; matrix products, arithmetic and copies ran while one was open for 14% of the time, Pallas kernels for 0%

commit v1 on v0

--- a/solution.py
+++ b/solution.py
@@ -111,12 +111,15 @@
         direction_core = direction
         residual_core = residual
         curvature, crossing, squares = lax.psum(
-            (
-                moments_local(direction_core, image_set),
-                moments_local(image_set, residual_core),
-                moments_local(image_set, image_set),
+            lax.psum(
+                (
+                    moments_local(direction_core, image_set),
+                    moments_local(image_set, residual_core),
+                    moments_local(image_set, image_set),
+                ),
+                "grp",
             ),
-            ("grp", "az", "ax"),
+            ("az", "ax"),
         )
         step_mix = solve_posdef(curvature, norms_now)
         norms_next = norms_now - jnp.dot(step_mix.T, crossing, precision=exact_mode)

time: 252 us -> 340 us (1.35)
  blocking collectives: 115 us -> 207 us
  starting transfers between devices: 31.1 us -> 26.9 us
    psum x0 -> x3, blocking collectives: none -> 146 us  [per_device(): lax.psum(lax.psum((moments_local(direction_core, image_set), moments_loca...]
    psum x2 -> x3, blocking collectives: 76.4 us -> 22.4 us  [per_device(): lax.psum((moments_local(direction_core, image_set), moments_local(image_s...]
    ppermute x6, starting transfers between devices: 11.4 us -> 16.4 us  [extended(): after = lax.ppermute(first, axis, down)]
    ppermute x6, starting transfers between devices: 13.6 us -> 8.64 us  [extended(): before = lax.ppermute(last, axis, up)]
    ppermute x3, starting transfers between devices: 6.13 us -> 1.85 us  [swapped(): return lax.ppermute(block, axis, route)]
    unnamed x50 -> x54, local copies, waits for them, and re-layouts: 12 us -> 12.8 us
  transfers between devices with their start and end apart: 15 -> 15, of which waited for: 2 -> 1; matrix products, arithmetic and copies ran while one was open for 14% -> 11% of each run, Pallas kernels for 0% -> 0%
where the time goes in v1:
time: 340 us; the launch traced here: 339 us
  blocking collectives  207 us (61%)
  local copies, waits for them, and re-layouts  37.6 us (11%)
  matrix products  35.8 us (11%)
  other arithmetic  29 us (9%)
  starting transfers between devices  26.9 us (8%)
    psum x3, blocking collectives, per_device(): lax.psum(lax.psum((moments_local(direction_core, image_set), moments_loca...  146 us
    psum x1, blocking collectives, per_device(): lax.psum(moments_local(start_core, start_core), ('grp', 'az', 'ax'))  38.4 us
    psum x3, blocking collectives, per_device(): lax.psum((moments_local(direction_core, image_set), moments_local(image_s...  22.4 us
    ppermute x6, starting transfers between devices, extended(): after = lax.ppermute(first, axis, down)  16.4 us
    dot_general x14, matrix products, products(): jnp.einsum('vrax,wrax->vw', first_set, second_set, precision=exact_mode)  14.9 us
    unnamed x54, local copies, waits for them, and re-layouts  12.8 us
    dot_general x8, matrix products, combine(): return jnp.einsum('vrax,vw->wrax', vector_set, mixing, precision=exact_mode)  9.04 us
    dot_general x3, matrix products, column_part(): jnp.einsum('rs,vsc->vrc', matrix, flat_set, precision=exact_mode)  8.66 us
  transfers between devices with their start and end apart: 15, of which 1 were waited for; matrix products, arithmetic and copies ran while one was open for 11% of the time, Pallas kernels for 0%

profile of v1, /device:TPU:0, one launch (start us, length us, event | category | flops | bytes accessed | tf_op | source)
XLA Modules:
  0.0 338.7 jit_solution(2520135641435191818)
XLA Ops:
  0.6 2.5 fusion.124
  5.1 2.4 collective-permute-start.3
  7.9 1.3 collective-permute-start.2
  9.2 2.4 collective-permute-start.1
  11.6 3.1 collective-permute-start
  16.1 1.6 collective-permute-start.4
  17.7 1.9 convolution_bitcast_fusion.3
  20.0 38.4 %psum.107 = f32[8,8]{0,1:T(8,128)S(1)} all-reduce(f32[8,8]{0,1:T(8,128)S(1)} %fusion.13), channel_id=1, replica_groups=mesh['grp'=2,'az'=8,'ax'=2] {'grp','az','ax'}, use_global_device_ids=true, to_apply=%region_4.0 | all-reduce | flops 64 | bytes 512 | tf_op jit(solution)/shard_map/psum | solution.py:108
  60.7 2.4 convolution_bitcast_fusion.2
  63.8 1.2 custom-call.19
  65.0 1.4 copy.167
  66.3 1.4 copy.165
  68.4 2.3 fusion.26
  72.9 1.9 convolution_bitcast_fusion.15
  74.8 1.8 convolution_bitcast_fusion.13
  77.2 8.9 %all-reduce.5 = (f32[8,8]{1,0:T(8,128)S(1)}, f32[8,8]{0,1:T(8,128)S(1)}, f32[8,8]{0,1:T(8,128)S(1)}) all-reduce(f32[8,8]{1,0:T(8,128)S(1)} %bitcast.241, f32[8,8]{0,1:T(8,128)S(1)} %fusion.11, f32[8,8]{0,1:T(8,128)S(1)} %fusion.9), channel_id=1, replica_groups=mesh['grp'=2,'az'=8,'ax'=2] {'grp'}, use_global_device_ids=true, to_apply=%region_0.1 | all-reduce | flops 192 | bytes 1536 | tf_op jit(solution)/shard_map/psum | solution.py:114
  86.1 57.8 %all-reduce.3 = (f32[8,8]{1,0:T(8,128)S(1)}, f32[8,8]{0,1:T(8,128)S(1)}, f32[8,8]{0,1:T(8,128)S(1)}) all-reduce(f32[8,8]{1,0:T(8,128)S(1)} %get-tuple-element.100, f32[8,8]{0,1:T(8,128)S(1)} %get-tuple-element.101, f32[8,8]{0,1:T(8,128)S(1)} %get-tuple-element.102), channel_id=1, replica_groups=mesh['grp'=2,'az'=8,'ax'=2] {'az','ax'}, use_global_device_ids=true, to_apply=%region_1.2 | all-reduce | flops 192 | bytes 1536 | tf_op jit(solution)/shard_map/psum | solution.py:113
  147.1 1.9 fusion.31
  152.4 1.2 fusion.121
  155.8 2.1 copy.206
  157.9 1.9 collective-permute-start.8
  160.8 1.3 collective-permute-start.7
  162.1 4.7 %collective-permute-start.5 = (f32[8,54,1,128]{3,0,1,2:T(8,128)}, f32[8,54,1,128]{3,0,1,2:T(8,128)}, u32[]{:S(2)}, u32[]{:S(2)}) collective-permute-start(f32[8,54,1,128]{3,0,1,2:T(8,128)} %get-tuple-element.111), channel_id=1, source_target_pairs={{2,0},{4,2},{6,4},{8,6},{10,8},{12,10},{14,12},{0,14},{3,1},{5,3},... | collective-permute-start | bytes 663560 | tf_op jit(solution)/shard_map/ppermute | solution.py:28
  166.8 3.1 convolution_bitcast_fusion.1
  172.9 1.2 custom-call.23
  174.1 1.1 copy.207
  175.2 1.4 copy.205
  177.3 2.5 fusion.22
  181.2 1.8 convolution_bitcast_fusion.11
  183.0 1.8 convolution_bitcast_fusion.9
  184.8 1.8 convolution_bitcast_fusion.7
  187.6 8.5 %all-reduce.4 = (f32[8,8]{0,1:T(8,128)S(1)}, f32[8,8]{0,1:T(8,128)S(1)}, f32[8,8]{0,1:T(8,128)S(1)}) all-reduce(f32[8,8]{0,1:T(8,128)S(1)} %fusion.7, f32[8,8]{0,1:T(8,128)S(1)} %fusion.5, f32[8,8]{0,1:T(8,128)S(1)} %fusion.3), channel_id=1, replica_groups=mesh['grp'=2,'az'=8,'ax'=2] {'grp'}, use_global_device_ids=true, to_apply=%region_9.13 | all-reduce | flops 192 | bytes 1536 | tf_op jit(solution)/shard_map/psum | solution.py:114
  196.1 57.8 %all-reduce.2 = (f32[8,8]{0,1:T(8,128)S(1)}, f32[8,8]{0,1:T(8,128)}, f32[8,8]{0,1:T(8,128)}) all-reduce(f32[8,8]{0,1:T(8,128)S(1)} %get-tuple-element.97, f32[8,8]{0,1:T(8,128)S(1)} %get-tuple-element.98, f32[8,8]{0,1:T(8,128)S(1)} %get-tuple-element.99), channel_id=1, replica_groups=mesh['grp'=2,'az'=8,'ax'=2] {'az','ax'}, use_global_device_ids=true, to_apply=%region_10.14 | all-reduce | flops 192 | bytes 1536 | tf_op jit(solution)/shard_map/psum | solution.py:113
  260.8 1.5 fusion.119
  264.2 1.9 convolution_add_fusion.2
  266.1 2.2 copy.237
  268.3 1.9 collective-permute-start.13
  271.2 1.3 collective-permute-start.12
  272.5 4.7 %collective-permute-start.10 = (f32[8,54,1,128]{3,0,1,2:T(8,128)}, f32[8,54,1,128]{3,0,1,2:T(8,128)}, u32[]{:S(2)}, u32[]{:S(2)}) collective-permute-start(f32[8,54,1,128]{3,0,1,2:T(8,128)} %get-tuple-element.105), channel_id=1, source_target_pairs={{2,0},{4,2},{6,4},{8,6},{10,8},{12,10},{14,12},{0,14},{3,1},{5,3},... | collective-permute-start | bytes 663560 | tf_op jit(solution)/shard_map/ppermute | solution.py:28
  277.2 3.1 convolution_bitcast_fusion
  281.1 1.1 copy.238
  282.3 1.4 copy.236
  284.4 1.4 collective-permute-done.10
  285.8 2.4 fusion.18
  289.7 1.8 convolution_bitcast_fusion.5
  291.8 5.0 %psum.118 = f32[8,8]{0,1:T(8,128)S(1)} all-reduce(f32[8,8]{0,1:T(8,128)S(1)} %fusion.1), channel_id=1, replica_groups=mesh['grp'=2,'az'=8,'ax'=2] {'grp'}, use_global_device_ids=true, to_apply=%region_15.19 | all-reduce | flops 64 | bytes 512 | tf_op jit(solution)/shard_map/psum | solution.py:114
  296.8 30.5 %psum.119 = f32[8,8]{0,1:T(8,128)S(1)} all-reduce(f32[8,8]{0,1:T(8,128)S(1)} %psum.118), channel_id=1, replica_groups=mesh['grp'=2,'az'=8,'ax'=2] {'az','ax'}, use_global_device_ids=true, to_apply=%region_16.20 | all-reduce | flops 64 | bytes 512 | tf_op jit(solution)/shard_map/psum | solution.py:113
  335.8 1.4 copy.250
  (173 shorter events, 49.3 us)
Async XLA Ops:
  0.6 2.5 copy-start.7
  5.1 59.9 %collective-permute-start.3 = (f32[8,54,4,1]{1,0,3,2:T(8,128)}, f32[8,54,4,1]{1,0,3,2:T(8,128)S(1)}, u32[]{:S(2)}, u32[]{:S(2)}) collective-permute-start(f32[8,54,4,1]{1,0,3,2:T(8,128)} %copy.166), channel_id=1, source_target_pairs={{0,1},{2,3},{4,5},{6,7},{8,9},{10,11},{12,13},{14,15},{16,17},{18,... | collective-permute-start | bytes 20744 | tf_op jit(solution)/shard_map/ppermute | solution.py:27
  7.5 10.2 %copy-start = (f32[8,48,4,128]{3,2,1,0:T(4,128)S(1)}, f32[8,48,4,128]{3,2,1,0:T(4,128)}, u32[]{:S(2)}) copy-start(f32[8,48,4,128]{3,2,1,0:T(4,128)} %param.24) | copy-start | bytes 2359300
  7.9 58.5 %collective-permute-start.2 = (f32[8,54,4,1]{1,0,3,2:T(8,128)S(1)}, f32[8,54,4,1]{1,0,3,2:T(8,128)S(1)}, u32[]{:S(2)}, u32[]{:S(2)}) collective-permute-start(f32[8,54,4,1]{1,0,3,2:T(8,128)S(1)} %copy.164), channel_id=1, source_target_pairs={{1,0},{3,2},{5,4},{7,6},{9,8},{11,10},{13,12},{15,14},{17,16},{19,... | collective-permute-start | bytes 20744 | tf_op jit(solution)/shard_map/ppermute | solution.py:28
  9.2 58.5 %collective-permute-start.1 = (f32[8,54,1,128]{3,0,1,2:T(8,128)S(1)}, f32[8,54,1,128]{3,0,1,2:T(8,128)S(1)}, u32[]{:S(2)}, u32[]{:S(2)}) collective-permute-start(f32[8,54,1,128]{3,0,1,2:T(8,128)S(1)} %get-tuple-element.116), channel_id=1, source_target_pairs={{0,2},{2,4},{4,6},{6,8},{8,10},{10,12},{12,14},{14,0},{1,3},{3,5},... | collective-permute-start | bytes 663560 | tf_op jit(solution)/shard_map/ppermute | solution.py:27
  11.6 56.8 %collective-permute-start = (f32[8,54,1,128]{3,0,1,2:T(8,128)S(1)}, f32[8,54,1,128]{3,0,1,2:T(8,128)}, u32[]{:S(2)}, u32[]{:S(2)}) collective-permute-start(f32[8,54,1,128]{3,0,1,2:T(8,128)S(1)} %get-tuple-element.115), channel_id=1, source_target_pairs={{2,0},{4,2},{6,4},{8,6},{10,8},{12,10},{14,12},{0,14},{3,1},{5,3},... | collective-permute-start | bytes 663560 | tf_op jit(solution)/shard_map/ppermute | solution.py:28
  16.1 54.7 %collective-permute-start.4 = (f32[8,2,4,128]{3,0,1,2:T(8,128)}, f32[8,2,4,128]{3,0,1,2:T(8,128)}, u32[]{:S(2)}, u32[]{:S(2)}) collective-permute-start(f32[8,2,4,128]{3,0,1,2:T(8,128)} %pad_maximum_fusion.12), channel_id=1, source_target_pairs={{0,16},{16,0},{1,17},{17,1},{2,18},{18,2},{3,19},{19,3},{4,20},{20... | collective-permute-start | bytes 98312 | tf_op jit(solution)/shard_map/ppermute | solution.py:17
  20.0 40.6 %copy-start.9 = (f32[1,48,48]{2,1,0:T(8,128)S(1)}, f32[1,48,48]{2,1,0:T(8,128)}, u32[]{:S(2)}) copy-start(f32[1,48,48]{2,1,0:T(8,128)} %param.26) | copy-start | bytes 27652
  59.9 0.7 copy-start.16
  60.6 2.4 copy-start.23
  60.6 2.4 copy-start.13
  60.6 2.4 copy-start.21
  63.8 4.6 %copy-start.1 = (f32[8,54,512]{2,1,0:T(8,128)S(1)}, f32[8,54,512]{2,1,0:T(8,128)}, u32[]{:S(2)}) copy-start(f32[8,54,512]{2,1,0:T(8,128)} %convolution_bitcast_fusion.2) | copy-start | bytes 2654212
  67.7 0.7 copy-start.10
  74.8 1.8 copy-start.8
  150.4 0.7 copy-start.17
  157.9 16.2 %collective-permute-start.8 = (f32[8,54,4,1]{1,0,3,2:T(8,128)}, f32[8,54,4,1]{1,0,3,2:T(8,128)}, u32[]{:S(2)}, u32[]{:S(2)}) collective-permute-start(f32[8,54,4,1]{1,0,3,2:T(8,128)} %copy.206), channel_id=1, source_target_pairs={{0,1},{2,3},{4,5},{6,7},{8,9},{10,11},{12,13},{14,15},{16,17},{18,... | collective-permute-start | bytes 20744 | tf_op jit(solution)/shard_map/ppermute | solution.py:27
  160.8 14.5 %collective-permute-start.7 = (f32[8,54,4,1]{1,0,3,2:T(8,128)}, f32[8,54,4,1]{1,0,3,2:T(8,128)S(1)}, u32[]{:S(2)}, u32[]{:S(2)}) collective-permute-start(f32[8,54,4,1]{1,0,3,2:T(8,128)} %copy.204), channel_id=1, source_target_pairs={{1,0},{3,2},{5,4},{7,6},{9,8},{11,10},{13,12},{15,14},{17,16},{19,... | collective-permute-start | bytes 20744 | tf_op jit(solution)/shard_map/ppermute | solution.py:28
  162.1 14.5 %collective-permute-start.6 = (f32[8,54,1,128]{3,0,1,2:T(8,128)}, f32[8,54,1,128]{3,0,1,2:T(8,128)S(1)}, u32[]{:S(2)}, u32[]{:S(2)}) collective-permute-start(f32[8,54,1,128]{3,0,1,2:T(8,128)} %get-tuple-element.112), channel_id=1, source_target_pairs={{0,2},{2,4},{4,6},{6,8},{8,10},{10,12},{12,14},{14,0},{1,3},{3,5},... | collective-permute-start | bytes 663560 | tf_op jit(solution)/shard_map/ppermute | solution.py:27
  162.1 15.2 %collective-permute-start.5 = (f32[8,54,1,128]{3,0,1,2:T(8,128)}, f32[8,54,1,128]{3,0,1,2:T(8,128)}, u32[]{:S(2)}, u32[]{:S(2)}) collective-permute-start(f32[8,54,1,128]{3,0,1,2:T(8,128)} %get-tuple-element.111), channel_id=1, source_target_pairs={{2,0},{4,2},{6,4},{8,6},{10,8},{12,10},{14,12},{0,14},{3,1},{5,3},... | collective-permute-start | bytes 663560 | tf_op jit(solution)/shard_map/ppermute | solution.py:28
  166.8 3.2 copy-start.14
  166.8 3.2 copy-start.15
  170.0 0.7 copy-start.19
  170.6 9.1 %collective-permute-start.9 = (f32[8,2,4,128]{3,0,1,2:T(8,128)}, f32[8,2,4,128]{3,0,1,2:T(8,128)}, u32[]{:S(2)}, u32[]{:S(2)}) collective-permute-start(f32[8,2,4,128]{3,0,1,2:T(8,128)} %pad_maximum_fusion.13), channel_id=1, source_target_pairs={{0,16},{16,0},{1,17},{17,1},{2,18},{18,2},{3,19},{19,3},{4,20},{20... | collective-permute-start | bytes 98312 | tf_op jit(solution)/shard_map/ppermute | solution.py:17
  176.6 0.7 copy-start.11
  257.0 0.9 copy-start.20
  258.0 0.7 copy-start.22
  258.8 0.7 copy-start.18
  263.0 1.2 copy-start.3
  266.1 4.1 %copy-start.2 = (f32[8,54,4,1]{3,0,1,2:T(8,128)S(1)}, f32[8,54,4,1]{3,0,1,2:T(8,128)}, u32[]{:S(2)}) copy-start(f32[8,54,4,1]{3,0,1,2:T(8,128)} %get-tuple-element.107) | copy-start | bytes 20740
  268.3 12.8 %collective-permute-start.13 = (f32[8,54,4,1]{1,0,3,2:T(8,128)}, f32[8,54,4,1]{1,0,3,2:T(8,128)}, u32[]{:S(2)}, u32[]{:S(2)}) collective-permute-start(f32[8,54,4,1]{1,0,3,2:T(8,128)} %copy.237), channel_id=1, source_target_pairs={{0,1},{2,3},{4,5},{6,7},{8,9},{10,11},{12,13},{14,15},{16,17},{18,... | collective-permute-start | bytes 20744 | tf_op jit(solution)/shard_map/ppermute | solution.py:27
  271.2 11.1 %collective-permute-start.12 = (f32[8,54,4,1]{1,0,3,2:T(8,128)}, f32[8,54,4,1]{1,0,3,2:T(8,128)S(1)}, u32[]{:S(2)}, u32[]{:S(2)}) collective-permute-start(f32[8,54,4,1]{1,0,3,2:T(8,128)} %copy.235), channel_id=1, source_target_pairs={{1,0},{3,2},{5,4},{7,6},{9,8},{11,10},{13,12},{15,14},{17,16},{19,... | collective-permute-start | bytes 20744 | tf_op jit(solution)/shard_map/ppermute | solution.py:28
  272.5 11.2 %collective-permute-start.11 = (f32[8,54,1,128]{3,0,1,2:T(8,128)}, f32[8,54,1,128]{3,0,1,2:T(8,128)S(1)}, u32[]{:S(2)}, u32[]{:S(2)}) collective-permute-start(f32[8,54,1,128]{3,0,1,2:T(8,128)} %get-tuple-element.106), channel_id=1, source_target_pairs={{0,2},{2,4},{4,6},{6,8},{8,10},{10,12},{12,14},{14,0},{1,3},{3,5},... | collective-permute-start | bytes 663560 | tf_op jit(solution)/shard_map/ppermute | solution.py:27
  272.5 13.3 %collective-permute-start.10 = (f32[8,54,1,128]{3,0,1,2:T(8,128)}, f32[8,54,1,128]{3,0,1,2:T(8,128)}, u32[]{:S(2)}, u32[]{:S(2)}) collective-permute-start(f32[8,54,1,128]{3,0,1,2:T(8,128)} %get-tuple-element.105), channel_id=1, source_target_pairs={{2,0},{4,2},{6,4},{8,6},{10,8},{12,10},{14,12},{0,14},{3,1},{5,3},... | collective-permute-start | bytes 663560 | tf_op jit(solution)/shard_map/ppermute | solution.py:28
  281.0 7.3 %collective-permute-start.14 = (f32[8,2,4,128]{3,0,1,2:T(8,128)}, f32[8,2,4,128]{3,0,1,2:T(8,128)}, u32[]{:S(2)}, u32[]{:S(2)}) collective-permute-start(f32[8,2,4,128]{3,0,1,2:T(8,128)} %pad_maximum_fusion.14), channel_id=1, source_target_pairs={{0,16},{16,0},{1,17},{17,1},{2,18},{18,2},{3,19},{19,3},{4,20},{20... | collective-permute-start | bytes 98312 | tf_op jit(solution)/shard_map/ppermute | solution.py:17
  283.7 0.7 copy-start.12
  330.5 1.2 copy-start.6
  331.7 1.8 copy-start.4
  332.5 1.0 copy-start.5
  333.5 1.1 slice-start.2
  334.6 1.2 slice-start
  335.8 1.4 slice-start.3
  337.2 0.9 slice-start.1
